TPU v7x, 32 devices: a whole 2x2x4 slice. The times are simulated.
32 devices in a mesh: row: 8 (over z, x), col: 2 (over y), rep: 2 (over core).
Axes of the slice: x: 2, y: 2, z: 4, core: 2. Of those that a mesh axis runs over, the one named last changes fastest.
Arguments:
- matrix: float32 [16384, 16384], P('row', 'col'), may hold values from -0.125 to 0.125
- vectors: float32 [64, 16384], P('rep', 'row'), may hold values from -0.3 to 0.3
Outputs:
- result: float32 [64, 16384], P('rep', 'row')
All inputs are finite; a program needn't handle non-finite values.
Results may differ from a plain program's by a relative error of at most 0.00011.
Values sent between devices are 32-bit elements; how exact they have to be, the bound alone decides.
A program may use at most 128 MiB of HBM per device.

v0:
```python
import jax
import jax.numpy as jnp
from jax import lax
from jax.sharding import PartitionSpec as P

TERMS = 6
STEPS = 1


def broadcast(block, axis, holder):
    block = jnp.where(lax.axis_index(axis) == holder, block, jnp.zeros_like(block))
    return lax.psum(block, axis)


def apply_matrix(current, matrix):
    fanout = lax.axis_size("row") // lax.axis_size("col")
    column_index = lax.axis_index("col")
    pieces = [broadcast(current, "row", column_index * fanout + which) for which in range(fanout)]
    operand = jnp.concatenate(pieces, axis=1)
    partial_value = lax.dot_general(
        operand,
        matrix,
        (((1,), (1,)), ((), ())),
        precision=lax.Precision.HIGHEST,
        preferred_element_type=jnp.float32,
    )
    return lax.psum(partial_value, "col")


def local(matrix, vectors):
    summand = vectors
    running = vectors
    for degree in range(1, TERMS + 1):
        summand = apply_matrix(summand, matrix) / float(degree * STEPS)
        running = running + summand
    return running


def solution(mesh):
    placed = (P("row", "col"), P("rep", "row"))
    return jax.shard_map(
        local, mesh=mesh, in_specs=placed, out_specs=P("rep", "row"), check_vma=False
    )
```

profile of v0, /device:TPU:0, one launch (start us, length us, event | category | flops | bytes accessed | tf_op | source)
XLA Modules:
  0.0 1029.5 jit_solution(9411824174395434742)
XLA Ops:
  6.5 1.9 broadcast_select_fusion.7
  8.5 0.0 all-reduce.19.cloned.1.call-start
  8.6 83.8 %all-reduce.41.cloned.1.call-done = (f32[32,2048]{1,0:T(8,128)}, f32[32,2048]{1,0:T(8,128)}, f32[32,2048]{1,0:T(8,128)}, f32[32,2048]{1,0:T(8,128)}) async-done(((f32[32,2048]{1,0:T(8,128)}, f32[32,2048]{1,0:T(8,128)}, f32[32,2048]{1,0:T(8,128)}, f32[32,2048]{1,0:T(8,128)}), (f32[32,2048]{1,0:T(8,128)}, f32[32,2048]{1,0:T(8,128)}, f32[32,2048]{1,0:T(8,128)}, ...) | async-done | bytes 1048592 | tf_op jit(solution)/shard_map/psum | solution.py:12
  92.4 63.2 %fusion = f32[32,2048]{1,0:T(8,128)} fusion(f32[2048,8192]{1,0:T(8,128)} %param.2, f32[32,2048]{1,0:T(8,128)} %get-tuple-element.25, f32[32,2048]{1,0:T(8,128)} %get-tuple-element.26, f32[32,2048]{1,0:T(8,128)} %get-tuple-element.27, f32[32,2048]{1,0:T(8,128)} %get-tuple-element.28), kind=kOutput, calls=%fused_computation | convolution fusion | flops 6443237376 | bytes 68419584 | tf_op jit(solution)/shard_map/dot_general | solution.py:20
  155.6 0.0 all-reduce.39.cloned.1.call-start
  155.7 22.8 %all-reduce.19.cloned.1.call-done = f32[32,2048]{1,0:T(8,128)} async-done(((f32[32,2048]{1,0:T(8,128)}), f32[32,2048]{1,0:T(8,128)}) %all-reduce.19.cloned.1.call-update) | async-done | bytes 262160 | tf_op jit(solution)/shard_map/psum | solution.py:27
  178.5 1.9 broadcast_select_fusion.3
  180.4 0.3 all-reduce.21.cloned.1.call-start
  180.8 80.1 %all-reduce.39.cloned.1.call-done = (f32[32,2048]{1,0:T(8,128)}, f32[32,2048]{1,0:T(8,128)}, f32[32,2048]{1,0:T(8,128)}, f32[32,2048]{1,0:T(8,128)}) async-done(((f32[32,2048]{1,0:T(8,128)}, f32[32,2048]{1,0:T(8,128)}, f32[32,2048]{1,0:T(8,128)}, f32[32,2048]{1,0:T(8,128)}), (f32[32,2048]{1,0:T(8,128)}, f32[32,2048]{1,0:T(8,128)}, f32[32,2048]{1,0:T(8,128)}, ...) | async-done | bytes 1048592 | tf_op jit(solution)/shard_map/psum | solution.py:12
  260.8 63.2 %fusion.8 = f32[32,2048]{1,0:T(8,128)} fusion(f32[2048,8192]{1,0:T(8,128)} %param.2, f32[32,2048]{1,0:T(8,128)} %get-tuple-element.21, f32[32,2048]{1,0:T(8,128)} %get-tuple-element.22, f32[32,2048]{1,0:T(8,128)} %get-tuple-element.23, f32[32,2048]{1,0:T(8,128)} %get-tuple-element.24), kind=kOutput, calls=%fused_computation.8 | convolution fusion | flops 6443237376 | bytes 68419584 | tf_op jit(solution)/shard_map/dot_general | solution.py:20
  324.1 22.8 %all-reduce.21.cloned.1.call-done = f32[32,2048]{1,0:T(8,128)} async-done(((f32[32,2048]{1,0:T(8,128)}), f32[32,2048]{1,0:T(8,128)}) %all-reduce.21.cloned.1.call-update) | async-done | bytes 262160 | tf_op jit(solution)/shard_map/psum | solution.py:27
  347.0 1.9 multiply_select_fusion.15
  349.0 80.1 %all-reduce.37.cloned.1.call-done = (f32[32,2048]{1,0:T(8,128)}, f32[32,2048]{1,0:T(8,128)}, f32[32,2048]{1,0:T(8,128)}, f32[32,2048]{1,0:T(8,128)}) async-done(((f32[32,2048]{1,0:T(8,128)}, f32[32,2048]{1,0:T(8,128)}, f32[32,2048]{1,0:T(8,128)}, f32[32,2048]{1,0:T(8,128)}), (f32[32,2048]{1,0:T(8,128)}, f32[32,2048]{1,0:T(8,128)}, f32[32,2048]{1,0:T(8,128)}, ...) | async-done | bytes 1048592 | tf_op jit(solution)/shard_map/psum | solution.py:12
  429.1 63.2 %fusion.16 = f32[32,2048]{1,0:T(8,128)} fusion(f32[2048,8192]{1,0:T(8,128)} %param.2, f32[32,2048]{1,0:T(8,128)} %get-tuple-element.17, f32[32,2048]{1,0:T(8,128)} %get-tuple-element.18, f32[32,2048]{1,0:T(8,128)} %get-tuple-element.19, f32[32,2048]{1,0:T(8,128)} %get-tuple-element.20), kind=kOutput, calls=%fused_computation.16 | convolution fusion | flops 6443237376 | bytes 68419584 | tf_op jit(solution)/shard_map/dot_general | solution.py:20
  492.3 0.6 all-reduce.35.cloned.1.call-start
  492.9 22.3 %all-reduce.23.cloned.1.call-done = f32[32,2048]{1,0:T(8,128)} async-done(((f32[32,2048]{1,0:T(8,128)}), f32[32,2048]{1,0:T(8,128)}) %all-reduce.23.cloned.1.call-update) | async-done | bytes 262160 | tf_op jit(solution)/shard_map/psum | solution.py:27
  515.2 2.0 multiply_select_fusion.11
  517.2 0.0 all-reduce.25.cloned.1.call-start
  517.2 80.3 %all-reduce.35.cloned.1.call-done = (f32[32,2048]{1,0:T(8,128)}, f32[32,2048]{1,0:T(8,128)}, f32[32,2048]{1,0:T(8,128)}, f32[32,2048]{1,0:T(8,128)}) async-done(((f32[32,2048]{1,0:T(8,128)}, f32[32,2048]{1,0:T(8,128)}, f32[32,2048]{1,0:T(8,128)}, f32[32,2048]{1,0:T(8,128)}), (f32[32,2048]{1,0:T(8,128)}, f32[32,2048]{1,0:T(8,128)}, f32[32,2048]{1,0:T(8,128)}, ...) | async-done | bytes 1048592 | tf_op jit(solution)/shard_map/psum | solution.py:12
  597.5 63.2 %fusion.24 = f32[32,2048]{1,0:T(8,128)} fusion(f32[2048,8192]{1,0:T(8,128)} %param.2, f32[32,2048]{1,0:T(8,128)} %get-tuple-element.13, f32[32,2048]{1,0:T(8,128)} %get-tuple-element.14, f32[32,2048]{1,0:T(8,128)} %get-tuple-element.15, f32[32,2048]{1,0:T(8,128)} %get-tuple-element.16), kind=kOutput, calls=%fused_computation.24 | convolution fusion | flops 6443237376 | bytes 68419584 | tf_op jit(solution)/shard_map/dot_general | solution.py:20
  660.8 22.8 %all-reduce.25.cloned.1.call-done = f32[32,2048]{1,0:T(8,128)} async-done(((f32[32,2048]{1,0:T(8,128)}), f32[32,2048]{1,0:T(8,128)}) %all-reduce.25.cloned.1.call-update) | async-done | bytes 262160 | tf_op jit(solution)/shard_map/psum | solution.py:27
  683.6 2.0 multiply_select_fusion.7
  685.6 0.2 all-reduce.27.cloned.1.call-start
  685.8 80.2 %all-reduce.33.cloned.1.call-done = (f32[32,2048]{1,0:T(8,128)}, f32[32,2048]{1,0:T(8,128)}, f32[32,2048]{1,0:T(8,128)}, f32[32,2048]{1,0:T(8,128)}) async-done(((f32[32,2048]{1,0:T(8,128)}, f32[32,2048]{1,0:T(8,128)}, f32[32,2048]{1,0:T(8,128)}, f32[32,2048]{1,0:T(8,128)}), (f32[32,2048]{1,0:T(8,128)}, f32[32,2048]{1,0:T(8,128)}, f32[32,2048]{1,0:T(8,128)}, ...) | async-done | bytes 1048592 | tf_op jit(solution)/shard_map/psum | solution.py:12
  766.0 63.2 %fusion.32 = f32[32,2048]{1,0:T(8,128)} fusion(f32[2048,8192]{1,0:T(8,128)} %param.2, f32[32,2048]{1,0:T(8,128)} %get-tuple-element.9, f32[32,2048]{1,0:T(8,128)} %get-tuple-element.10, f32[32,2048]{1,0:T(8,128)} %get-tuple-element.11, f32[32,2048]{1,0:T(8,128)} %get-tuple-element.12), kind=kOutput, calls=%fused_computation.32 | convolution fusion | flops 6443237376 | bytes 68419584 | tf_op jit(solution)/shard_map/dot_general | solution.py:20
  829.3 22.8 %all-reduce.27.cloned.1.call-done = f32[32,2048]{1,0:T(8,128)} async-done(((f32[32,2048]{1,0:T(8,128)}), f32[32,2048]{1,0:T(8,128)}) %all-reduce.27.cloned.1.call-update) | async-done | bytes 262160 | tf_op jit(solution)/shard_map/psum | solution.py:27
  852.2 2.0 multiply_select_fusion.3
  854.2 0.3 all-reduce.29.cloned.1.call-start
  854.5 80.1 %all-reduce.31.cloned.1.call-done = (f32[32,2048]{1,0:T(8,128)}, f32[32,2048]{1,0:T(8,128)}, f32[32,2048]{1,0:T(8,128)}, f32[32,2048]{1,0:T(8,128)}) async-done(((f32[32,2048]{1,0:T(8,128)}, f32[32,2048]{1,0:T(8,128)}, f32[32,2048]{1,0:T(8,128)}, f32[32,2048]{1,0:T(8,128)}), (f32[32,2048]{1,0:T(8,128)}, f32[32,2048]{1,0:T(8,128)}, f32[32,2048]{1,0:T(8,128)}, ...) | async-done | bytes 1048592 | tf_op jit(solution)/shard_map/psum | solution.py:12
  934.5 63.2 %fusion.40 = f32[32,2048]{1,0:T(8,128)} fusion(f32[2048,8192]{1,0:T(8,128)} %param.2, f32[32,2048]{1,0:T(8,128)} %get-tuple-element.5, f32[32,2048]{1,0:T(8,128)} %get-tuple-element.6, f32[32,2048]{1,0:T(8,128)} %get-tuple-element.7, f32[32,2048]{1,0:T(8,128)} %get-tuple-element.8), kind=kOutput, calls=%fused_computation.40 | convolution fusion | flops 6443237376 | bytes 68419584 | tf_op jit(solution)/shard_map/dot_general | solution.py:20
  997.8 22.9 %all-reduce.29.cloned.1.call-done = f32[32,2048]{1,0:T(8,128)} async-done(((f32[32,2048]{1,0:T(8,128)}), f32[32,2048]{1,0:T(8,128)}) %all-reduce.29.cloned.1.call-update) | async-done | bytes 262160 | tf_op jit(solution)/shard_map/psum | solution.py:27
  1020.7 1.8 multiply_add_fusion
  (29 shorter events, 0.4 us)
Async XLA Ops:
  6.5 85.8 %all-reduce.41.cloned.1.call-start = ((), (), s32[]{:S(2)}) async-start(), calls=%async_computation.11 | async-start | bytes 2097152 | tf_op jit(solution)/shard_map/psum | solution.py:12
  8.5 170.0 %all-reduce.19.cloned.1.call-start = ((), (), s32[]{:S(2)}) async-start(), calls=%async_computation | async-start | bytes 524288 | tf_op jit(solution)/shard_map/psum | solution.py:27
  155.6 105.2 %all-reduce.39.cloned.1.call-start = ((), (), s32[]{:S(2)}) async-start(), calls=%async_computation.10 | async-start | bytes 2097152 | tf_op jit(solution)/shard_map/psum | solution.py:12
  180.4 166.5 %all-reduce.21.cloned.1.call-start = ((), (), s32[]{:S(2)}) async-start(), calls=%async_computation.1 | async-start | bytes 524288 | tf_op jit(solution)/shard_map/psum | solution.py:27
  324.1 105.0 %all-reduce.37.cloned.1.call-start = ((), (), s32[]{:S(2)}) async-start(), calls=%async_computation.9 | async-start | bytes 2097152 | tf_op jit(solution)/shard_map/psum | solution.py:12
  348.9 166.3 %all-reduce.23.cloned.1.call-start = ((), (), s32[]{:S(2)}) async-start(), calls=%async_computation.2 | async-start | bytes 524288 | tf_op jit(solution)/shard_map/psum | solution.py:27
  492.3 105.2 %all-reduce.35.cloned.1.call-start = ((), (), s32[]{:S(2)}) async-start(), calls=%async_computation.8 | async-start | bytes 2097152 | tf_op jit(solution)/shard_map/psum | solution.py:12
  517.2 166.5 %all-reduce.25.cloned.1.call-start = ((), (), s32[]{:S(2)}) async-start(), calls=%async_computation.3 | async-start | bytes 524288 | tf_op jit(solution)/shard_map/psum | solution.py:27
  660.8 105.2 %all-reduce.33.cloned.1.call-start = ((), (), s32[]{:S(2)}) async-start(), calls=%async_computation.7 | async-start | bytes 2097152 | tf_op jit(solution)/shard_map/psum | solution.py:12
  685.6 166.5 %all-reduce.27.cloned.1.call-start = ((), (), s32[]{:S(2)}) async-start(), calls=%async_computation.4 | async-start | bytes 524288 | tf_op jit(solution)/shard_map/psum | solution.py:27
  829.2 191.4 %copy-start = (f32[32,2048]{1,0:T(8,128)S(1)}, f32[32,2048]{1,0:T(8,128)}, u32[]{:S(2)}) copy-start(f32[32,2048]{1,0:T(8,128)} %param.3) | copy-start | bytes 786436
  829.2 191.4 %copy-start.1 = (f32[32,2048]{1,0:T(8,128)S(1)}, f32[32,2048]{1,0:T(8,128)}, u32[]{:S(2)}) copy-start(f32[32,2048]{1,0:T(8,128)} %all-reduce.19.cloned.1.call-done) | copy-start | bytes 786436
  829.2 191.4 %copy-start.2 = (f32[32,2048]{1,0:T(8,128)S(1)}, f32[32,2048]{1,0:T(8,128)}, u32[]{:S(2)}) copy-start(f32[32,2048]{1,0:T(8,128)} %all-reduce.21.cloned.1.call-done) | copy-start | bytes 786436
  829.2 191.4 %copy-start.3 = (f32[32,2048]{1,0:T(8,128)S(1)}, f32[32,2048]{1,0:T(8,128)}, u32[]{:S(2)}) copy-start(f32[32,2048]{1,0:T(8,128)} %all-reduce.23.cloned.1.call-done) | copy-start | bytes 786436
  829.2 191.4 %copy-start.4 = (f32[32,2048]{1,0:T(8,128)S(1)}, f32[32,2048]{1,0:T(8,128)}, u32[]{:S(2)}) copy-start(f32[32,2048]{1,0:T(8,128)} %all-reduce.25.cloned.1.call-done) | copy-start | bytes 786436
  829.3 105.2 %all-reduce.31.cloned.1.call-start = ((), (), s32[]{:S(2)}) async-start(), calls=%async_computation.6 | async-start | bytes 2097152 | tf_op jit(solution)/shard_map/psum | solution.py:12
  852.2 168.5 %copy-start.5 = (f32[32,2048]{1,0:T(8,128)S(1)}, f32[32,2048]{1,0:T(8,128)}, u32[]{:S(2)}) copy-start(f32[32,2048]{1,0:T(8,128)} %all-reduce.27.cloned.1.call-done) | copy-start | bytes 786436
  854.2 166.4 %all-reduce.29.cloned.1.call-start = ((), (), s32[]{:S(2)}) async-start(), calls=%async_computation.5 | async-start | bytes 524288 | tf_op jit(solution)/shard_map/psum | solution.py:27
Sparse Core Ops, SparseCore 0:
  11.2 81.1 all-reduce.40
  155.7 22.7 all-reduce.18
  182.3 78.4 all-reduce.38
  324.2 22.7 all-reduce.20
  350.7 78.3 all-reduce.36
  492.4 22.7 all-reduce.22
  519.0 78.4 all-reduce.34
  660.9 22.7 all-reduce.24
  687.5 78.4 all-reduce.32
  829.4 22.7 all-reduce.26
  856.0 78.4 all-reduce.30
  997.9 22.7 all-reduce.28
where the time goes:
time: 1030 us
  waiting for transfers between devices  621 us (60%)
  matrix products  379 us (37%)
  between operations  13.8 us (1%)
  other arithmetic  13.5 us (1%)
    psum x6, waiting for transfers between devices, broadcast(): return lax.psum(block, axis)  484 us
    dot_general x6, matrix products, apply_matrix(): lax.dot_general(operand, matrix, (((1,), (1,)), ((), ())), precision=lax....  379 us
    psum x6, waiting for transfers between devices, apply_matrix(): return lax.psum(partial_value, 'col')  136 us
  transfers between devices with their start and end apart: 12, of which 12 were waited for; matrix products, arithmetic and copies ran while one was open for 0% of the time, Pallas kernels for 0%

commit v1 on v0

--- a/solution.py
+++ b/solution.py
@@ -24,7 +24,7 @@
         precision=lax.Precision.HIGHEST,
         preferred_element_type=jnp.float32,
     )
-    return lax.psum(partial_value, "col")
+    return jnp.sum(lax.all_gather(partial_value, "col"), axis=0)
 
 
 def local(matrix, vectors):

time: 1030 us -> 941 us (0.914)
  waiting for transfers between devices: 621 us -> 475 us
  blocking collectives: 0 us -> 48.3 us
  matrix products: 379 us -> 390 us
    psum x6 -> x0, waiting for transfers between devices: 136 us -> none  [apply_matrix(): return lax.psum(partial_value, 'col')]
    all_gather x0 -> x6, blocking collectives: none -> 48.3 us  [apply_matrix(): return jnp.sum(lax.all_gather(partial_value, 'col'), axis=0)]
    dot_general x6, matrix products: 379 us -> 390 us  [apply_matrix(): lax.dot_general(operand, matrix, (((1,), (1,)), ((), ())), precision=lax....]
  transfers between devices with their start and end apart: 12 -> 6, of which waited for: 12 -> 6; matrix products, arithmetic and copies ran while one was open for 0% -> 0% of each run, Pallas kernels for 0% -> 0%
where the time goes in v1:
time: 941 us; the launch traced here: 936 us
  waiting for transfers between devices  475 us (50%)
  matrix products  390 us (41%)
  blocking collectives  48.3 us (5%)
  between operations  13.9 us (1%)
    psum x6, waiting for transfers between devices, broadcast(): return lax.psum(block, axis)  475 us
    dot_general x6, matrix products, apply_matrix(): lax.dot_general(operand, matrix, (((1,), (1,)), ((), ())), precision=lax....  390 us
    all_gather x6, blocking collectives, apply_matrix(): return jnp.sum(lax.all_gather(partial_value, 'col'), axis=0)  48.3 us
  transfers between devices with their start and end apart: 6, of which 6 were waited for; matrix products, arithmetic and copies ran while one was open for 0% of the time, Pallas kernels for 0%

profile of v1, /device:TPU:0, one launch (start us, length us, event | category | flops | bytes accessed | tf_op | source)
XLA Modules:
  0.0 935.8 jit_solution(674097937612160043)
XLA Ops:
  6.5 1.9 broadcast_select_fusion.7
  8.5 0.0 all-reduce.23.cloned.1.call-update
  8.5 0.0 all-reduce.21.cloned.1.call-start
  8.5 83.8 %all-reduce.23.cloned.1.call-done = (f32[32,2048]{1,0:T(8,128)}, f32[32,2048]{1,0:T(8,128)}, f32[32,2048]{1,0:T(8,128)}, f32[32,2048]{1,0:T(8,128)}) async-done(((f32[32,2048]{1,0:T(8,128)}, f32[32,2048]{1,0:T(8,128)}, f32[32,2048]{1,0:T(8,128)}, f32[32,2048]{1,0:T(8,128)}), (f32[32,2048]{1,0:T(8,128)}, f32[32,2048]{1,0:T(8,128)}, f32[32,2048]{1,0:T(8,128)}, ...) | async-done | bytes 1048592 | tf_op jit(solution)/shard_map/psum | solution.py:12
  92.4 65.0 %fusion = f32[32,2048]{1,0:T(8,128)S(1)} fusion(f32[2048,8192]{1,0:T(8,128)} %param.2, f32[32,2048]{1,0:T(8,128)} %get-tuple-element.25, f32[32,2048]{1,0:T(8,128)} %get-tuple-element.26, f32[32,2048]{1,0:T(8,128)} %get-tuple-element.27, f32[32,2048]{1,0:T(8,128)} %get-tuple-element.28), kind=kOutput, calls=%fused_computation | convolution fusion | flops 6443237376 | bytes 68419584 | tf_op jit(solution)/shard_map/dot_general | solution.py:20
  157.4 8.0 all-gather
  165.4 1.0 broadcast_select_fusion.3
  166.4 0.0 all-reduce.21.cloned.1.call-update
  166.4 0.2 all-reduce.19.cloned.1.call-start
  166.7 78.1 %all-reduce.21.cloned.1.call-done = (f32[32,2048]{1,0:T(8,128)}, f32[32,2048]{1,0:T(8,128)}, f32[32,2048]{1,0:T(8,128)}, f32[32,2048]{1,0:T(8,128)}) async-done(((f32[32,2048]{1,0:T(8,128)}, f32[32,2048]{1,0:T(8,128)}, f32[32,2048]{1,0:T(8,128)}, f32[32,2048]{1,0:T(8,128)}), (f32[32,2048]{1,0:T(8,128)}, f32[32,2048]{1,0:T(8,128)}, f32[32,2048]{1,0:T(8,128)}, ...) | async-done | bytes 1048592 | tf_op jit(solution)/shard_map/psum | solution.py:12
  244.8 65.0 %fusion.8 = f32[32,2048]{1,0:T(8,128)S(1)} fusion(f32[2048,8192]{1,0:T(8,128)} %param.2, f32[32,2048]{1,0:T(8,128)} %get-tuple-element.21, f32[32,2048]{1,0:T(8,128)} %get-tuple-element.22, f32[32,2048]{1,0:T(8,128)} %get-tuple-element.23, f32[32,2048]{1,0:T(8,128)} %get-tuple-element.24), kind=kOutput, calls=%fused_computation.8 | convolution fusion | flops 6443237376 | bytes 68419584 | tf_op jit(solution)/shard_map/dot_general | solution.py:20
  309.8 8.0 all-gather.1
  317.8 1.0 multiply_select_fusion.15
  318.8 0.0 all-reduce.17.cloned.1.call-start
  318.9 78.2 %all-reduce.19.cloned.1.call-done = (f32[32,2048]{1,0:T(8,128)}, f32[32,2048]{1,0:T(8,128)}, f32[32,2048]{1,0:T(8,128)}, f32[32,2048]{1,0:T(8,128)}) async-done(((f32[32,2048]{1,0:T(8,128)}, f32[32,2048]{1,0:T(8,128)}, f32[32,2048]{1,0:T(8,128)}, f32[32,2048]{1,0:T(8,128)}), (f32[32,2048]{1,0:T(8,128)}, f32[32,2048]{1,0:T(8,128)}, f32[32,2048]{1,0:T(8,128)}, ...) | async-done | bytes 1048592 | tf_op jit(solution)/shard_map/psum | solution.py:12
  397.1 65.0 %fusion.16 = f32[32,2048]{1,0:T(8,128)S(1)} fusion(f32[2048,8192]{1,0:T(8,128)} %param.2, f32[32,2048]{1,0:T(8,128)} %get-tuple-element.17, f32[32,2048]{1,0:T(8,128)} %get-tuple-element.18, f32[32,2048]{1,0:T(8,128)} %get-tuple-element.19, f32[32,2048]{1,0:T(8,128)} %get-tuple-element.20), kind=kOutput, calls=%fused_computation.16 | convolution fusion | flops 6443237376 | bytes 68419584 | tf_op jit(solution)/shard_map/dot_general | solution.py:20
  462.2 8.2 all-gather.2
  470.4 1.0 multiply_select_fusion.11
  471.5 0.0 all-reduce.15.cloned.1.call-start
  471.5 78.3 %all-reduce.17.cloned.1.call-done = (f32[32,2048]{1,0:T(8,128)}, f32[32,2048]{1,0:T(8,128)}, f32[32,2048]{1,0:T(8,128)}, f32[32,2048]{1,0:T(8,128)}) async-done(((f32[32,2048]{1,0:T(8,128)}, f32[32,2048]{1,0:T(8,128)}, f32[32,2048]{1,0:T(8,128)}, f32[32,2048]{1,0:T(8,128)}), (f32[32,2048]{1,0:T(8,128)}, f32[32,2048]{1,0:T(8,128)}, f32[32,2048]{1,0:T(8,128)}, ...) | async-done | bytes 1048592 | tf_op jit(solution)/shard_map/psum | solution.py:12
  549.8 65.0 %fusion.24 = f32[32,2048]{1,0:T(8,128)S(1)} fusion(f32[2048,8192]{1,0:T(8,128)} %param.2, f32[32,2048]{1,0:T(8,128)} %get-tuple-element.13, f32[32,2048]{1,0:T(8,128)} %get-tuple-element.14, f32[32,2048]{1,0:T(8,128)} %get-tuple-element.15, f32[32,2048]{1,0:T(8,128)} %get-tuple-element.16), kind=kOutput, calls=%fused_computation.24 | convolution fusion | flops 6443237376 | bytes 68419584 | tf_op jit(solution)/shard_map/dot_general | solution.py:20
  614.8 8.0 all-gather.3
  622.8 1.0 multiply_select_fusion.7
  623.9 0.0 all-reduce.13.cloned.1.call-start
  623.9 78.2 %all-reduce.15.cloned.1.call-done = (f32[32,2048]{1,0:T(8,128)}, f32[32,2048]{1,0:T(8,128)}, f32[32,2048]{1,0:T(8,128)}, f32[32,2048]{1,0:T(8,128)}) async-done(((f32[32,2048]{1,0:T(8,128)}, f32[32,2048]{1,0:T(8,128)}, f32[32,2048]{1,0:T(8,128)}, f32[32,2048]{1,0:T(8,128)}), (f32[32,2048]{1,0:T(8,128)}, f32[32,2048]{1,0:T(8,128)}, f32[32,2048]{1,0:T(8,128)}, ...) | async-done | bytes 1048592 | tf_op jit(solution)/shard_map/psum | solution.py:12
  702.1 65.0 %fusion.32 = f32[32,2048]{1,0:T(8,128)S(1)} fusion(f32[2048,8192]{1,0:T(8,128)} %param.2, f32[32,2048]{1,0:T(8,128)} %get-tuple-element.9, f32[32,2048]{1,0:T(8,128)} %get-tuple-element.10, f32[32,2048]{1,0:T(8,128)} %get-tuple-element.11, f32[32,2048]{1,0:T(8,128)} %get-tuple-element.12), kind=kOutput, calls=%fused_computation.32 | convolution fusion | flops 6443237376 | bytes 68419584 | tf_op jit(solution)/shard_map/dot_general | solution.py:20
  767.2 8.1 all-gather.4
  775.4 1.0 multiply_select_fusion.3
  776.4 78.3 %all-reduce.13.cloned.1.call-done = (f32[32,2048]{1,0:T(8,128)}, f32[32,2048]{1,0:T(8,128)}, f32[32,2048]{1,0:T(8,128)}, f32[32,2048]{1,0:T(8,128)}) async-done(((f32[32,2048]{1,0:T(8,128)}, f32[32,2048]{1,0:T(8,128)}, f32[32,2048]{1,0:T(8,128)}, f32[32,2048]{1,0:T(8,128)}), (f32[32,2048]{1,0:T(8,128)}, f32[32,2048]{1,0:T(8,128)}, f32[32,2048]{1,0:T(8,128)}, ...) | async-done | bytes 1048592 | tf_op jit(solution)/shard_map/psum | solution.py:12
  854.7 65.0 %fusion.40 = f32[32,2048]{1,0:T(8,128)S(1)} fusion(f32[2048,8192]{1,0:T(8,128)} %param.2, f32[32,2048]{1,0:T(8,128)} %get-tuple-element.5, f32[32,2048]{1,0:T(8,128)} %get-tuple-element.6, f32[32,2048]{1,0:T(8,128)} %get-tuple-element.7, f32[32,2048]{1,0:T(8,128)} %get-tuple-element.8), kind=kOutput, calls=%fused_computation.40 | convolution fusion | flops 6443237376 | bytes 68419584 | tf_op jit(solution)/shard_map/dot_general | solution.py:20
  919.7 8.0 all-gather.5
  927.8 0.8 multiply_add_fusion
  (13 shorter events, 0.3 us)
Async XLA Ops:
  6.5 85.8 %all-reduce.23.cloned.1.call-start = ((), (), s32[]{:S(2)}) async-start(), calls=%async_computation.5 | async-start | bytes 2097152 | tf_op jit(solution)/shard_map/psum | solution.py:12
  8.5 236.3 %all-reduce.21.cloned.1.call-start = ((), (), s32[]{:S(2)}) async-start(), calls=%async_computation.4 | async-start | bytes 2097152 | tf_op jit(solution)/shard_map/psum | solution.py:12
  166.4 230.7 %all-reduce.19.cloned.1.call-start = ((), (), s32[]{:S(2)}) async-start(), calls=%async_computation.3 | async-start | bytes 2097152 | tf_op jit(solution)/shard_map/psum | solution.py:12
  318.8 230.9 %all-reduce.17.cloned.1.call-start = ((), (), s32[]{:S(2)}) async-start(), calls=%async_computation.2 | async-start | bytes 2097152 | tf_op jit(solution)/shard_map/psum | solution.py:12
  471.5 230.7 %all-reduce.15.cloned.1.call-start = ((), (), s32[]{:S(2)}) async-start(), calls=%async_computation.1 | async-start | bytes 2097152 | tf_op jit(solution)/shard_map/psum | solution.py:12
  623.9 230.8 %all-reduce.13.cloned.1.call-start = ((), (), s32[]{:S(2)}) async-start(), calls=%async_computation | async-start | bytes 2097152 | tf_op jit(solution)/shard_map/psum | solution.py:12
  767.2 160.6 %copy-start = (f32[32,2048]{1,0:T(8,128)S(1)}, f32[32,2048]{1,0:T(8,128)}, u32[]{:S(2)}) copy-start(f32[32,2048]{1,0:T(8,128)} %param.3) | copy-start | bytes 786436
Sparse Core Ops, SparseCore 0:
  11.2 81.1 all-reduce.22
  166.6 78.1 all-reduce.20
  319.0 78.1 all-reduce.18
  471.6 78.1 all-reduce.16
  624.0 78.1 all-reduce.14
  776.5 78.1 all-reduce.12
